TPU v7x, 32 devices: a whole 2x2x4 slice. The times are simulated.
32 devices in a mesh: dp: 8 (over z, y), tr: 2 (over core), tc: 2 (over x).
Axes of the slice: x: 2, y: 2, z: 4, core: 2. Of those that a mesh axis runs over, the one named last changes fastest.
Arguments:
- activations: bfloat16 [4096, 4096], P('dp', ('tr', 'tc')), may hold values from -16.8 to 16.8, as said below
- gradients: bfloat16 [4096, 7168], P('dp', ('tr', 'tc')), may hold values from -16.8 to 16.8, as said below
- old_inputs: float32 [4096, 4096], P(('dp', 'tr', 'tc')), may hold values from -3 to 3
- old_gradients: float32 [7168, 7168], P(('dp', 'tr', 'tc')), may hold values from -3 to 3
Outputs:
- input_factor: float32 [4096, 4096], P(('dp', 'tr', 'tc'))
- grad_factor: float32 [7168, 7168], P(('dp', 'tr', 'tc'))
Inputs may be any that keep to these rules, and one draw needn't show every extreme that they name: `activations`: real-valued samples. `gradients`: real-valued samples.
All inputs are finite; a program needn't handle non-finite values.
Results may differ from a plain program's by a relative error of at most 0.0045.
Values may be sent and summed in bfloat16 or wider, within the bound.
A program may use at most 192 MiB of HBM per device.

v0:
```python
import functools

import jax
import jax.numpy as jnp
from jax import lax
from jax.experimental import pallas as pl
from jax.experimental.pallas import tpu as pltpu
from jax.sharding import Mesh, PartitionSpec as P

GROUP = (2, 2, 2)
REPLICA = ("q", "zh", "zl", "y")
AXES = REPLICA + ("tr", "tc")
F32, BF16 = jnp.float32, jnp.bfloat16
LANES, STEP = 128, 256
VMEM, WIDE_VMEM = 54 * 2**20, 55 * 2**20
CHUNKS = (4, 2)


def split_mesh(mesh):
    size = mesh.shape["dp"] // 8
    rest = tuple(mesh.shape[name] for name in mesh.axis_names[1:])
    return Mesh(mesh.devices.reshape((size,) + GROUP + rest), AXES)


class Place:
    def __init__(self):
        for name in AXES:
            setattr(self, name, lax.axis_index(name))
        self.replica = self.zh * 4 + self.zl * 2 + self.y
        self.partner = self.zh * 4 + (1 - self.zl) * 2 + self.y

        self.cell = self.tr * 2 + self.tc

    def flip(self, *names):
        return {name: 1 - getattr(self, name) for name in names}


class Factor:
    def __init__(self, at, chunks, groups, each, samples, old, total, refs):
        self.at, self.chunks, self.groups, self.each = at, chunks, groups, each
        self.samples, self.old, self.total = samples, old, total
        (self.wide, self.left, self.left_in, self.pair, self.pair_in, self.sum, self.done,
         self.done_in, self.local_sem, self.send_sem, self.recv_sem, self.ready) = refs
        self.tokens, self.width = samples.shape
        self.lines = self.pair.shape[0]
        self.rows = self.lines // 4
        self.fold = groups == 1
        self.turn = lax.rem(at.tc + at.zl, 2)
        steps = self.width // STEP
        self.parts = ((0, (steps + 1) // 2), ((steps + 1) // 2, steps))
        keys = [("far", k) for k in range(chunks)]
        keys += [("y", t, k) for t in range(2) for k in range(chunks)]
        keys += [(n, t, o) for n in ("cross", "give", "pass") for t in range(2) for o in range(2)]
        keys += [("pair", p) for p in range(2)]
        keys += [("done", p, f) for p in range(2) for f in range(3)]
        keys += [("mix", s, i) for s in range(2) for i in range(2)]
        self.keys = {key: i for i, key in enumerate(keys)}
        self.sent = {}

    def copy(self, key, source, target, device):
        at = self.keys[key]
        return pltpu.make_async_remote_copy(
            src_ref=source,
            dst_ref=target,
            send_sem=self.send_sem.at[at],
            recv_sem=self.recv_sem.at[at],
            device_id=device,
            device_id_type=pl.DeviceIdType.MESH,
        )

    def start(self, key, source, target, device):
        self.sent[key] = self.copy(key, source, target, device)
        self.sent[key].start()

    def leave(self, *key):
        self.sent.pop(key).wait_send()

    def receive(self, key, here):
        self.copy(key, here, here, self.at.flip("tr")).wait_recv()

    def spot(self, t, y, k):
        size = self.tokens // self.chunks
        return self.wide.at[pl.ds(pl.multiple_of((2 * t + y) * self.tokens + k * size, size), size)]

    def own(self, k):
        size = self.tokens // self.chunks
        return self.samples.at[pl.ds(k * size, size)]

    def local(self):
        row = pl.multiple_of(self.at.y * self.tokens, self.tokens)
        target = self.wide.at[pl.ds(row, self.tokens)]
        copies = [pltpu.make_async_copy(self.samples, target, self.local_sem.at[0])]
        if self.fold:
            copies.append(pltpu.make_async_copy(self.old, self.total, self.local_sem.at[1]))
        return copies

    def far(self):
        for k in range(self.chunks):
            self.start(("far", k), self.own(k), self.spot(1, self.at.y, k), self.at.flip("zh"))

    def far_left(self):
        for k in range(self.chunks):
            self.leave("far", k)

    def beside(self, t, k):
        here = self.spot(t, self.at.y, k)
        self.start(("y", t, k), here if t else self.own(k), here, self.at.flip("y"))

    def beside_own(self):
        for k in range(self.chunks):
            self.beside(0, k)

    def beside_left(self):
        for t in range(2):
            for k in range(self.chunks):
                self.leave("y", t, k)

    def beside_far(self):
        for k in range(self.chunks):
            self.receive(("far", k), self.spot(1, self.at.y, k))
            self.beside(1, k)

    def beside_wait(self, t):
        for k in range(self.chunks):
            self.receive(("y", t, k), self.spot(t, 1 - self.at.y, k))

    def stretch(self, t, o):
        y = 1 - self.at.y if o else self.at.y
        return pl.ds(pl.multiple_of((2 * t + y) * self.tokens, self.tokens), self.tokens)

    def pick(self, s, replica, tokens):
        at, rows, each = self.at, self.rows, self.each
        span = 4 * each
        window = span if span % LANES == 0 else -(-span // LANES) * LANES + LANES
        line = lax.broadcasted_iota(jnp.int32, (rows, window), 0)
        feature = lax.broadcasted_iota(jnp.int32, (rows, window), 1)
        total = 0.0
        for group in range(self.groups):
            offset = (group * 8 + replica) * span - at.cell * self.width
            start = pl.multiple_of(jnp.clip(offset // LANES * LANES, 0, self.width - window), LANES)
            cells = []
            for cell in range(4):
                hit = feature == line + (offset - start + (cell - group) * each)
                if self.groups > 1:
                    hit &= (line >= group * each) & (line < (group + 1) * each)
                cells.append(jnp.where(hit, 1.0, 0.0).astype(BF16))
            total += lax.dot_general(
                jnp.concatenate(cells, axis=0),
                self.wide[tokens, pl.ds(start, window)],
                (((1,), (1,)), ((), ())),
                preferred_element_type=F32,
            )
        self.left[s, :, tokens] = total.astype(BF16)

    def give(self, t, o):
        if self.groups > 1:
            return
        at, tokens = self.at, self.stretch(t, o)
        self.pick(self.turn, jnp.where(self.turn == 0, at.replica, at.partner), tokens)
        here = self.left.at[self.turn, :, tokens]
        self.start(("cross", t, o), here, here, at.flip("tc"))
        self.start(("give", t, o), here, here, at.flip("tr"))

    def hand_on(self, t, o):
        if self.groups > 1:
            return
        here = self.left.at[1 - self.turn, :, self.stretch(t, o)]
        self.receive(("cross", t, o), here)
        self.start(("pass", t, o), here, here, self.at.flip("tr"))

    def get_left(self, lead):
        at = self.at
        if self.groups == 1:
            if not lead:
                for t in range(2):
                    for o in range(2):
                        self.receive(("give", t, o), self.left.at[self.turn, :, self.stretch(t, o)])
                        self.receive(("pass", t, o), self.left.at[1 - self.turn, :, self.stretch(t, o)])
            return
        for s, replica in ((0, at.replica), (1, at.partner)):
            def block(b, carry, s=s, replica=replica):
                tokens = pl.ds(pl.multiple_of(b * self.tokens, self.tokens), self.tokens)
                self.pick(s, replica, tokens)
                return carry

            lax.fori_loop(0, 4, block, 0)
        for s in range(2):
            for i, name in enumerate(("tr", "tc")):
                other = at.flip(name)
                pl.semaphore_signal(self.ready.at[i], inc=1, device_id=other, device_id_type=pl.DeviceIdType.MESH)
                pl.semaphore_wait(self.ready.at[i], 1)
                self.start(("mix", s, i), self.left.at[s], self.left_in, other)
                self.receive(("mix", s, i), self.left_in)
                self.leave("mix", s, i)
                self.left[s] = self.left[s] + self.left_in[...]

    def columns(self, part):
        low, high = self.parts[part]
        return pl.ds(low * STEP, (high - low) * STEP)

    def steps(self, part, one):
        low, high = self.parts[part]

        def step(i, carry):
            one(pl.ds(pl.multiple_of(i * STEP, STEP), STEP), i)
            return carry

        lax.fori_loop(low, high, step, 0)

    def product(self, s, columns):
        return jnp.dot(self.left[s], self.wide[:, columns], preferred_element_type=F32)

    def pair_products(self, scale):
        def one(columns, i):
            self.pair[:, columns] = (self.product(1, columns) * scale).astype(BF16)

        for part in range(2):
            self.steps(part, one)
            here = self.columns(part)
            self.start(("pair", part), self.pair.at[:, here], self.pair_in.at[:, here], self.at.flip("zl"))

    def own_products(self, scale):
        def one(columns, i):
            self.sum[:, columns] = self.product(0, columns) * scale

        for part in range(2):
            self.steps(part, one)

    def others(self):
        at = self.at
        for f, (up, over) in enumerate(((0, 1), (1, 0), (1, 1))):
            tr = 1 - at.tr if up else at.tr
            tc = 1 - at.tc if over else at.tc
            yield f, {"tr": tr, "tc": tc}, tr * 2 + tc

    def lot(self, cell):
        return pl.ds(pl.multiple_of(cell * self.rows, 16), self.rows)

    def put(self, cell, i, value):
        place = pl.ds(pl.multiple_of(cell * self.width + i * STEP, LANES), STEP)
        self.total[:, place] = 0.5 * self.total[:, place] + 0.5 * value if self.fold else value

    def spread(self):
        at = self.at

        def one(columns, i):
            value = self.sum[:, columns] + self.pair_in[:, columns].astype(F32)
            self.sum[:, columns] = value
            self.done[:, columns] = value.astype(BF16)
            self.put(at.cell, i, self.sum[self.lot(at.cell), columns])

        for part in range(2):
            here = self.columns(part)
            self.receive(("pair", part), self.pair_in.at[:, here])
            self.steps(part, one)
            for f, device, cell in self.others():
                self.start(
                    ("done", part, f),
                    self.done.at[self.lot(cell), here],
                    self.done_in.at[self.lot(at.cell), here],
                    device,
                )

    def finish(self):
        for part in range(2):
            for f, device, cell in self.others():
                def one(columns, i, cell=cell):
                    self.put(cell, i, self.done_in[self.lot(cell), columns].astype(F32))

                self.receive(("done", part, f), self.done_in.at[self.lot(cell), self.columns(part)])
                self.steps(part, one)

    def drain(self):
        for key in list(self.sent):
            self.leave(*key)


def program(lead, at, g, a, scale, flags):
    def tell(i):
        pl.semaphore_signal(flags.at[i], inc=1, device_id=at.flip("tr"), device_id_type=pl.DeviceIdType.MESH)

    def hear(i):
        pl.semaphore_wait(flags.at[i], 1)

    local = g.local() + a.local()
    if not lead:
        g.far()
    for copy in local:
        copy.start()
    if lead:
        g.beside_own()
        local.pop(0).wait()
        g.give(0, 0)
        g.beside_wait(0)
        g.give(0, 1)
        g.beside_far()
        g.give(1, 0)
        hear(1)
        g.far()
        g.beside_left()
        tell(0)
        g.hand_on(0, 0)
        g.hand_on(0, 1)
        g.beside_wait(1)
        g.give(1, 1)
        for copy in local:
            copy.wait()
        a.beside_own()
        a.give(0, 0)
        g.hand_on(1, 0)
        g.hand_on(1, 1)
        g.get_left(lead)
        g.pair_products(scale)
        g.own_products(scale)
        g.far_left()
        tell(3)
        a.beside_wait(0)
        a.give(0, 1)
        hear(2)
        a.far()
        a.beside_far()
        a.give(1, 0)
        a.hand_on(0, 0)
        a.hand_on(0, 1)
        a.beside_wait(1)
        a.give(1, 1)
        a.hand_on(1, 0)
        a.hand_on(1, 1)
        a.get_left(lead)
        a.pair_products(scale)
        g.spread()
        a.own_products(scale)
    else:
        g.far_left()
        tell(1)
        hear(0)
        g.beside_own()
        for copy in local:
            copy.wait()
        g.beside_far()
        hear(3)
        a.far()
        a.beside_own()
        g.beside_wait(0)
        g.beside_wait(1)
        g.get_left(lead)
        g.pair_products(scale)
        a.far_left()
        tell(2)
        g.own_products(scale)
        a.beside_far()
        a.beside_wait(0)
        a.beside_wait(1)
        a.get_left(lead)
        a.pair_products(scale)
        a.own_products(scale)
        g.spread()
    g.finish()
    a.spread()
    a.finish()
    g.drain()
    a.drain()


def kernel(groups, each, scale, *refs):
    at = Place()
    barrier = pltpu.get_barrier_semaphore()
    peers = [at.flip(name) for name in ("tc", "y", "zh", "tr", "zl")] + [at.flip("tr", "tc")]
    for peer in peers:
        pl.semaphore_signal(barrier, inc=1, device_id=peer, device_id_type=pl.DeviceIdType.MESH)
    pl.semaphore_wait(barrier, len(peers))

    samples, refs = refs[:2], refs[2:]
    olds = (None, None)
    if groups == 1:
        olds, refs = refs[:2], refs[2:]
    totals, scratch, flags = refs[:2], refs[2:-1], refs[-1]
    count = len(scratch) // 2

    def run(lead):
        factors = [
            Factor(at, CHUNKS[i], groups, each[i], samples[i], olds[i], totals[i],
                   scratch[i * count:(i + 1) * count])
            for i in range(2)
        ]
        program(lead, at, *factors, scale, flags)

    lead = at.tr == at.zh
    pl.when(lead)(functools.partial(run, True))
    pl.when(jnp.logical_not(lead))(functools.partial(run, False))


def scratch_of(samples, rows, groups, chunks):
    tokens, width = samples.shape
    lines = 4 * rows
    copies = 3 * chunks + 24
    return [
        pltpu.VMEM((4 * tokens, width), BF16),
        pltpu.VMEM((2, lines, 4 * tokens), BF16),
        pltpu.VMEM((lines, 4 * tokens) if groups > 1 else (16, LANES), BF16),
        pltpu.VMEM((lines, width), BF16),
        pltpu.VMEM((lines, width), BF16),
        pltpu.VMEM((lines, width), F32),
        pltpu.VMEM((lines, width), BF16),
        pltpu.VMEM((lines, width), BF16),
        pltpu.SemaphoreType.DMA((2,)),
        pltpu.SemaphoreType.DMA((copies,)),
        pltpu.SemaphoreType.DMA((copies,)),
        pltpu.SemaphoreType.REGULAR((2,)),
    ]


def body(activations, gradients, old_inputs, old_gradients):
    groups = lax.axis_size("q")
    tokens = activations.shape[0] * lax.axis_size(REPLICA)
    samples, olds = (gradients, activations), (old_gradients, old_inputs)
    each = tuple(old.shape[0] for old in olds)
    scratch = []
    for block, rows, chunks in zip(samples, each, CHUNKS):
        scratch += scratch_of(block, groups * rows, groups, chunks)
    scratch.append(pltpu.SemaphoreType.REGULAR((4,)))
    operands = samples + olds if groups == 1 else samples
    new = pl.pallas_call(
        functools.partial(kernel, groups, each, 1.0 / tokens),
        out_shape=tuple(
            pltpu.VMEM((groups * old.shape[0], old.shape[1]), F32) for old in olds
        ),
        in_specs=[pl.BlockSpec(memory_space=pltpu.HBM)] * len(operands),
        out_specs=(pl.BlockSpec(memory_space=pltpu.VMEM),) * 2,
        scratch_shapes=scratch,
        compiler_params=pltpu.CompilerParams(
            collective_id=0,
            has_side_effects=True,
            vmem_limit_bytes=VMEM if groups == 1 else WIDE_VMEM,
        ),
        name="gram",
    )(*operands)
    if groups > 1:
        new = [lax.psum_scatter(total, "q", scatter_dimension=0, tiled=True) for total in new]
        new = [0.5 * old + 0.5 * total for total, old in zip(new, olds)]
    return new[1], new[0]


def solution(mesh):
    rows = REPLICA + ("tr", "tc")
    return jax.shard_map(
        body,
        mesh=split_mesh(mesh),
        in_specs=(
            P(REPLICA, ("tr", "tc")),
            P(REPLICA, ("tr", "tc")),
            P(rows, None),
            P(rows, None),
        ),
        out_specs=(P(rows, None), P(rows, None)),
        check_vma=False,
    )
```

profile of v0, /device:TPU:1, one launch (start us, length us, event | category | flops | bytes accessed | tf_op | source)
XLA Modules:
  0.0 216.5 jit_solution(3584057250740278640)
XLA Ops:
  0.6 211.8 %gram.1 = (f32[224,7168]{1,0:T(8,128)S(1)}, f32[128,4096]{1,0:T(8,128)S(1)}) custom-call(bf16[512,1792]{1,0:T(8,128)(2,1)} %refs_0_.1, bf16[512,1024]{1,0:T(8,128)(2,1)} %refs_1_.1, f32[224,7168]{1,0:T(8,128)} %refs_2_.1, f32[128,4096]{1,0:T(8,128)} %refs_3_.1), custom_call_target="tpu_custom_call" | custom-call | tf_op jit(solution)/shard_map/gram/pallas_call | solution.py:423
  212.4 1.3 copy.8
  213.7 2.7 %copy.9 = f32[224,7168]{1,0:T(8,128)} copy(f32[224,7168]{1,0:T(8,128)S(1)} %get-tuple-element.7) | data formatting | bytes 12845056
where the time goes:
time: 217 us; the launch traced here: 216 us
  Pallas kernels  212 us (98%)
  local copies, waits for them, and re-layouts  4.07 us (2%)
    pallas_call x1, Pallas kernels, body(): pl.pallas_call(functools.partial(kernel, groups, each, 1.0 / tokens), out...  212 us

commit v1 on v0

--- a/solution.py
+++ b/solution.py
@@ -12,7 +12,9 @@
 AXES = REPLICA + ("tr", "tc")
 F32, BF16 = jnp.float32, jnp.bfloat16
 LANES, STEP = 128, 256
-VMEM, WIDE_VMEM = 54 * 2**20, 55 * 2**20
+VMEM, WIDE_VMEM = 54 * 2**20, 223 * 2**18
+PARTS = 4
+PIECES = tuple((t, o, i) for t in range(2) for o in range(2) for i in range(2))
 CHUNKS = (4, 2)
 
 
@@ -47,12 +49,13 @@
         self.fold = groups == 1
         self.turn = lax.rem(at.tc + at.zl, 2)
         steps = self.width // STEP
-        self.parts = ((0, (steps + 1) // 2), ((steps + 1) // 2, steps))
+        each_part = -(-steps // PARTS)
+        self.parts = tuple((low, min(low + each_part, steps)) for low in range(0, steps, each_part))
         keys = [("far", k) for k in range(chunks)]
         keys += [("y", t, k) for t in range(2) for k in range(chunks)]
-        keys += [(n, t, o) for n in ("cross", "give", "pass") for t in range(2) for o in range(2)]
-        keys += [("pair", p) for p in range(2)]
-        keys += [("done", p, f) for p in range(2) for f in range(3)]
+        keys += [(n,) + piece for n in ("cross", "give", "pass") for piece in PIECES]
+        keys += [("pair", p) for p in range(len(self.parts))]
+        keys += [("done", p, f) for p in range(len(self.parts)) for f in range(3)]
         keys += [("mix", s, i) for s in range(2) for i in range(2)]
         self.keys = {key: i for i, key in enumerate(keys)}
         self.sent = {}
@@ -115,18 +118,29 @@
             for k in range(self.chunks):
                 self.leave("y", t, k)
 
-    def beside_far(self):
-        for k in range(self.chunks):
-            self.receive(("far", k), self.spot(1, self.at.y, k))
-            self.beside(1, k)
+    def beside_far(self, lead):
+        each = self.chunks // 2
+        for i in range(2):
+            for k in range(i * each, (i + 1) * each):
+                self.receive(("far", k), self.spot(1, self.at.y, k))
+                self.beside(1, k)
+            if lead:
+                self.give(1, 0, i)
 
     def beside_wait(self, t):
         for k in range(self.chunks):
             self.receive(("y", t, k), self.spot(t, 1 - self.at.y, k))
 
-    def stretch(self, t, o):
-        y = 1 - self.at.y if o else self.at.y
-        return pl.ds(pl.multiple_of((2 * t + y) * self.tokens, self.tokens), self.tokens)
+    def beside_give(self, t):
+        each = self.chunks // 2
+        for i in range(2):
+            for k in range(i * each, (i + 1) * each):
+                self.receive(("y", t, k), self.spot(t, 1 - self.at.y, k))
+            self.give(t, 1, i)
+
+    def stretch(self, t, o, i):
+        y, size = 1 - self.at.y if o else self.at.y, self.tokens // 2
+        return pl.ds(pl.multiple_of((2 * t + y) * self.tokens + i * size, size), size)
 
     def pick(self, s, replica, tokens):
         at, rows, each = self.at, self.rows, self.each
@@ -152,30 +166,34 @@
             )
         self.left[s, :, tokens] = total.astype(BF16)
 
-    def give(self, t, o):
+    def give(self, t, o, i):
         if self.groups > 1:
             return
-        at, tokens = self.at, self.stretch(t, o)
+        at, tokens = self.at, self.stretch(t, o, i)
         self.pick(self.turn, jnp.where(self.turn == 0, at.replica, at.partner), tokens)
         here = self.left.at[self.turn, :, tokens]
-        self.start(("cross", t, o), here, here, at.flip("tc"))
-        self.start(("give", t, o), here, here, at.flip("tr"))
+        self.start(("cross", t, o, i), here, here, at.flip("tc"))
+        self.start(("give", t, o, i), here, here, at.flip("tr"))
+
+    def give_own(self):
+        for i in range(2):
+            self.give(0, 0, i)
 
     def hand_on(self, t, o):
         if self.groups > 1:
             return
-        here = self.left.at[1 - self.turn, :, self.stretch(t, o)]
-        self.receive(("cross", t, o), here)
-        self.start(("pass", t, o), here, here, self.at.flip("tr"))
+        for i in range(2):
+            here = self.left.at[1 - self.turn, :, self.stretch(t, o, i)]
+            self.receive(("cross", t, o, i), here)
+            self.start(("pass", t, o, i), here, here, self.at.flip("tr"))
 
     def get_left(self, lead):
         at = self.at
         if self.groups == 1:
             if not lead:
-                for t in range(2):
-                    for o in range(2):
-                        self.receive(("give", t, o), self.left.at[self.turn, :, self.stretch(t, o)])
-                        self.receive(("pass", t, o), self.left.at[1 - self.turn, :, self.stretch(t, o)])
+                for piece in PIECES:
+                    self.receive(("give",) + piece, self.left.at[self.turn, :, self.stretch(*piece)])
+                    self.receive(("pass",) + piece, self.left.at[1 - self.turn, :, self.stretch(*piece)])
             return
         for s, replica in ((0, at.replica), (1, at.partner)):
             def block(b, carry, s=s, replica=replica):
@@ -192,7 +210,13 @@
                 self.start(("mix", s, i), self.left.at[s], self.left_in, other)
                 self.receive(("mix", s, i), self.left_in)
                 self.leave("mix", s, i)
-                self.left[s] = self.left[s] + self.left_in[...]
+
+                def add(b, carry, s=s):
+                    tokens = pl.ds(pl.multiple_of(b * self.tokens, self.tokens), self.tokens)
+                    self.left[s, :, tokens] += self.left_in[:, tokens]
+                    return carry
+
+                lax.fori_loop(0, 4, add, 0)
 
     def columns(self, part):
         low, high = self.parts[part]
@@ -200,12 +224,11 @@
 
     def steps(self, part, one):
         low, high = self.parts[part]
-
-        def step(i, carry):
-            one(pl.ds(pl.multiple_of(i * STEP, STEP), STEP), i)
-            return carry
-
-        lax.fori_loop(low, high, step, 0)
+        lax.fori_loop(low, high, functools.partial(self.step, one), 0)
+
+    def step(self, one, i, carry):
+        one(pl.ds(pl.multiple_of(i * STEP, STEP), STEP), i)
+        return carry
 
     def product(self, s, columns):
         return jnp.dot(self.left[s], self.wide[:, columns], preferred_element_type=F32)
@@ -214,7 +237,7 @@
         def one(columns, i):
             self.pair[:, columns] = (self.product(1, columns) * scale).astype(BF16)
 
-        for part in range(2):
+        for part in range(len(self.parts)):
             self.steps(part, one)
             here = self.columns(part)
             self.start(("pair", part), self.pair.at[:, here], self.pair_in.at[:, here], self.at.flip("zl"))
@@ -223,8 +246,7 @@
         def one(columns, i):
             self.sum[:, columns] = self.product(0, columns) * scale
 
-        for part in range(2):
-            self.steps(part, one)
+        lax.fori_loop(0, self.width // STEP, functools.partial(self.step, one), 0)
 
     def others(self):
         at = self.at
@@ -249,7 +271,7 @@
             self.done[:, columns] = value.astype(BF16)
             self.put(at.cell, i, self.sum[self.lot(at.cell), columns])
 
-        for part in range(2):
+        for part in range(len(self.parts)):
             here = self.columns(part)
             self.receive(("pair", part), self.pair_in.at[:, here])
             self.steps(part, one)
@@ -262,7 +284,7 @@
                 )
 
     def finish(self):
-        for part in range(2):
+        for part in range(len(self.parts)):
             for f, device, cell in self.others():
                 def one(columns, i, cell=cell):
                     self.put(cell, i, self.done_in[self.lot(cell), columns].astype(F32))
@@ -290,23 +312,20 @@
     if lead:
         g.beside_own()
         local.pop(0).wait()
-        g.give(0, 0)
-        g.beside_wait(0)
-        g.give(0, 1)
-        g.beside_far()
-        g.give(1, 0)
+        g.give_own()
+        g.beside_give(0)
+        g.beside_far(lead)
+        g.beside_give(1)
+        g.beside_left()
+        tell(0)
         hear(1)
         g.far()
-        g.beside_left()
-        tell(0)
         g.hand_on(0, 0)
         g.hand_on(0, 1)
-        g.beside_wait(1)
-        g.give(1, 1)
         for copy in local:
             copy.wait()
         a.beside_own()
-        a.give(0, 0)
+        a.give_own()
         g.hand_on(1, 0)
         g.hand_on(1, 1)
         g.get_left(lead)
@@ -314,16 +333,13 @@
         g.own_products(scale)
         g.far_left()
         tell(3)
-        a.beside_wait(0)
-        a.give(0, 1)
+        a.beside_give(0)
         hear(2)
         a.far()
-        a.beside_far()
-        a.give(1, 0)
+        a.beside_far(lead)
         a.hand_on(0, 0)
         a.hand_on(0, 1)
-        a.beside_wait(1)
-        a.give(1, 1)
+        a.beside_give(1)
         a.hand_on(1, 0)
         a.hand_on(1, 1)
         a.get_left(lead)
@@ -337,7 +353,7 @@
         g.beside_own()
         for copy in local:
             copy.wait()
-        g.beside_far()
+        g.beside_far(lead)
         hear(3)
         a.far()
         a.beside_own()
@@ -348,7 +364,7 @@
         a.far_left()
         tell(2)
         g.own_products(scale)
-        a.beside_far()
+        a.beside_far(lead)
         a.beside_wait(0)
         a.beside_wait(1)
         a.get_left(lead)
@@ -393,7 +409,7 @@
 def scratch_of(samples, rows, groups, chunks):
     tokens, width = samples.shape
     lines = 4 * rows
-    copies = 3 * chunks + 24
+    copies = 3 * chunks + len(PIECES) * 3 + 4 * PARTS + 4
     return [
         pltpu.VMEM((4 * tokens, width), BF16),
         pltpu.VMEM((2, lines, 4 * tokens), BF16),

time: 217 us -> 209 us (0.963)
  the two profiles are of different devices: /device:TPU:1 before, /device:TPU:17 now
where the time goes in v1:
time: 209 us; the launch traced here: 207 us
  Pallas kernels  202 us (97%)
  local copies, waits for them, and re-layouts  4.07 us (2%)
    pallas_call x1, Pallas kernels, body(): pl.pallas_call(functools.partial(kernel, groups, each, 1.0 / tokens), out...  202 us

profile of v1, /device:TPU:17, one launch (start us, length us, event | category | flops | bytes accessed | tf_op | source)
XLA Modules:
  0.0 207.0 jit_solution(8147976054405405889)
XLA Ops:
  0.6 202.3 %gram.1 = (f32[224,7168]{1,0:T(8,128)S(1)}, f32[128,4096]{1,0:T(8,128)S(1)}) custom-call(bf16[512,1792]{1,0:T(8,128)(2,1)} %refs_0_.1, bf16[512,1024]{1,0:T(8,128)(2,1)} %refs_1_.1, f32[224,7168]{1,0:T(8,128)} %refs_2_.1, f32[128,4096]{1,0:T(8,128)} %refs_3_.1), custom_call_target="tpu_custom_call" | custom-call | tf_op jit(solution)/shard_map/gram/pallas_call | solution.py:439
  202.9 1.3 copy.8
  204.2 2.7 %copy.9 = f32[224,7168]{1,0:T(8,128)} copy(f32[224,7168]{1,0:T(8,128)S(1)} %get-tuple-element.7) | data formatting | bytes 12845056

commit v2 on v1

--- a/solution.py
+++ b/solution.py
@@ -50,7 +50,9 @@
         self.turn = lax.rem(at.tc + at.zl, 2)
         steps = self.width // STEP
         each_part = -(-steps // PARTS)
-        self.parts = tuple((low, min(low + each_part, steps)) for low in range(0, steps, each_part))
+        first = steps - (steps - 1) // each_part * each_part
+        ends = tuple(range(first, steps + 1, each_part))
+        self.parts = tuple(zip((0,) + ends, ends))
         keys = [("far", k) for k in range(chunks)]
         keys += [("y", t, k) for t in range(2) for k in range(chunks)]
         keys += [(n,) + piece for n in ("cross", "give", "pass") for piece in PIECES]
@@ -307,10 +309,11 @@
     local = g.local() + a.local()
     if not lead:
         g.far()
+    if lead:
+        g.beside_own()
     for copy in local:
         copy.start()
     if lead:
-        g.beside_own()
         local.pop(0).wait()
         g.give_own()
         g.beside_give(0)

time: 209 us -> 207 us (level)
  no operation moved by 1% of the time
where the time goes in v2:
time: 207 us; the launch traced here: 206 us
  Pallas kernels  201 us (97%)
  local copies, waits for them, and re-layouts  4.07 us (2%)
    pallas_call x1, Pallas kernels, body(): pl.pallas_call(functools.partial(kernel, groups, each, 1.0 / tokens), out...  201 us

profile of v2, /device:TPU:17, one launch (start us, length us, event | category | flops | bytes accessed | tf_op | source)
XLA Modules:
  0.0 205.8 jit_solution(14011767175470107533)
XLA Ops:
  0.6 201.1 %gram.1 = (f32[224,7168]{1,0:T(8,128)S(1)}, f32[128,4096]{1,0:T(8,128)S(1)}) custom-call(bf16[512,1792]{1,0:T(8,128)(2,1)} %refs_0_.1, bf16[512,1024]{1,0:T(8,128)(2,1)} %refs_1_.1, f32[224,7168]{1,0:T(8,128)} %refs_2_.1, f32[128,4096]{1,0:T(8,128)} %refs_3_.1), custom_call_target="tpu_custom_call" | custom-call | tf_op jit(solution)/shard_map/gram/pallas_call | solution.py:442
  201.7 1.3 copy.8
  203.0 2.7 %copy.9 = f32[224,7168]{1,0:T(8,128)} copy(f32[224,7168]{1,0:T(8,128)S(1)} %get-tuple-element.7) | data formatting | bytes 12845056
